TPU v7x, 512 devices: a whole 4x8x8 slice. The times are simulated.
512 devices in a mesh: gx: 64 (over x, y, core), ta: 8 (over z).
Axes of the slice: x: 4, y: 8, z: 8, core: 2. Of those that a mesh axis runs over, the one named last changes fastest.
Arguments:
- master_flat: float32 [8388608], P(('gx', 'ta')), may hold values from -6 to 6
Outputs:
- serving_weight: bfloat16 [1, 8192, 1024], P(None, None, 'ta')
- channel_scale: float32 [1, 1024], P(None, 'ta')
All inputs are finite; a program needn't handle non-finite values.
Results may differ from a plain program's by a relative error of at most 0.015.
Values may be sent and summed in bfloat16 or wider, within the bound.
No kernel may reach another device: no remote copies, remote signals or barrier semaphores. Data moves between devices by JAX's collectives and lax.ppermute only.
A program may use at most 64 MiB of HBM per device.

v0:
```python
import jax
import jax.numpy as jnp
from jax import lax
from jax.sharding import PartitionSpec as P

D = 8192
KVH = 8
HEAD = 128
LAYERS = 1


def relayout(shard):
    regrouped = lax.all_to_all(shard, "ta", split_axis=1, concat_axis=0, tiled=True)
    complete = lax.all_gather(regrouped, "gx", axis=0, tiled=True)
    return complete.reshape(LAYERS, D, -1)


def shards(master_flat):
    kv_width = KVH * HEAD
    row_count = master_flat.shape[0] // kv_width
    rounded = master_flat.reshape(row_count, kv_width).astype(jnp.bfloat16)
    complete = relayout(rounded)
    widened = complete.astype(jnp.float32)
    channel_scale = jnp.max(jnp.abs(widened), axis=1)
    serving_weight = (widened / channel_scale[:, None, :]).astype(jnp.bfloat16)
    return (serving_weight, channel_scale)


def solution(mesh):
    in_specs = (P(("gx", "ta")),)
    out_specs = (P(None, None, "ta"), P(None, "ta"))
    return jax.shard_map(shards, mesh=mesh, in_specs=in_specs, out_specs=out_specs, check_vma=False)
```

profile of v0, /device:TPU:1, one launch (start us, length us, event | category | flops | bytes accessed | tf_op | source)
XLA Modules:
  0.0 117.4 jit_solution(15112434270394180846)
XLA Ops:
  7.2 0.0 all-gather.2.cloned.1.call-start
  7.2 0.8 convert_bitcast_fusion
  8.1 17.5 %all_to_all.16 = bf16[16,8,128]{2,0,1:T(8,128)(2,1)} all-to-all(bf16[16,8,128]{2,0,1:T(8,128)(2,1)S(1)} %copy.4), channel_id=1, replica_groups=mesh['gx'=64,'ta'=8] {'ta'}, dimensions={1} | all-to-all | bytes 65536 | tf_op jit(solution)/shard_map/all_to_all | solution.py:13
  25.5 0.0 all-gather.2.cloned.1.call-update
  25.6 81.0 %all-gather.2.cloned.1.call-done = bf16[8192,128]{1,0:T(8,128)(2,1)} async-done(((bf16[128,128]{1,0:T(8,128)(2,1)}), bf16[8192,128]{1,0:T(8,128)(2,1)}) %all-gather.2.cloned.1.call-update) | async-done | bytes 2097168 | tf_op jit(solution)/shard_map/all_gather | solution.py:14
  106.6 0.0 copy-start
  106.6 2.0 %fusion = f32[128]{0:T(128)S(1)} fusion(bf16[8192,128]{1,0:T(8,128)(2,1)} %all-gather.2.cloned.1.call-done), kind=kLoop, calls=%fused_computation.2 | loop fusion | flops 3145600 | bytes 2097664 | tf_op jit(solution)/shard_map/reduce_max | solution.py:24
  108.6 0.2 copy-done
  108.8 0.0 copy-start.1
  108.8 1.7 %fusion.2 = bf16[1,8192,128]{2,1,0:T(8,128)(2,1)} fusion(bf16[8192,128]{1,0:T(8,128)(2,1)S(1)} %copy-done, f32[128]{0:T(128)S(1)} %fusion), kind=kLoop, calls=%fused_computation.4 | loop fusion | flops 3145728 | bytes 4194816 | tf_op jit(solution)/shard_map/convert_element_type | solution.py:25
  110.5 0.0 copy-done.1
  (1 shorter events, 0.0 us)
Async XLA Ops:
  7.2 99.4 %all-gather.2.cloned.1.call-start = ((), (), s32[]{:S(2)}) async-start(), calls=%async_computation.1 | async-start | bytes 2129920 | tf_op jit(solution)/shard_map/all_gather | solution.py:14
  106.6 2.2 %copy-start = (bf16[8192,128]{1,0:T(8,128)(2,1)S(1)}, bf16[8192,128]{1,0:T(8,128)(2,1)}, u32[]{:S(2)}) copy-start(bf16[8192,128]{1,0:T(8,128)(2,1)} %all-gather.2.cloned.1.call-done) | copy-start | bytes 6291460
  108.8 1.7 %copy-start.1 = (f32[128]{0:T(128)}, f32[128]{0:T(128)S(1)}, u32[]{:S(2)}) copy-start(f32[128]{0:T(128)S(1)} %fusion) | copy-start | bytes 1540
Sparse Core Ops, SparseCore 0:
  25.7 80.8 all-gather.1
where the time goes:
time: 118 us; the launch traced here: 117 us
  waiting for transfers between devices  81 us (69%)
  blocking collectives  17.5 us (15%)
  between operations  14 us (12%)
  other arithmetic  4.6 us (4%)
    all_gather x1, waiting for transfers between devices, relayout(): complete = lax.all_gather(regrouped, 'gx', axis=0, tiled=True)  81 us
    all_to_all x1, blocking collectives, relayout(): lax.all_to_all(shard, 'ta', split_axis=1, concat_axis=0, tiled=True)  17.5 us
  transfers between devices with their start and end apart: 1, of which 1 were waited for; matrix products, arithmetic and copies ran while one was open for 0% of the time, Pallas kernels for 0%

commit v1 on v0

v1 whole, which is shorter than its diff:
```python
import jax
import jax.numpy as jnp
from jax import lax
from jax.sharding import Mesh, PartitionSpec as P

D = 8192
KVH = 8
HEAD = 128
LAYERS = 1
AXES = ("x", "yh", "yl", "c", "ta")


def exchange(block, peers, axes):
    copies = jnp.broadcast_to(block[None], (peers,) + block.shape)
    return lax.all_to_all(copies, axes, 0, 0, tiled=True)


def shards(master_flat):
    rounded = master_flat.astype(jnp.bfloat16).reshape(16, 8, 128)
    by_channel = jnp.transpose(rounded, (1, 0, 2))
    copies = jnp.broadcast_to(by_channel[None], (4, 8, 16, 128)).reshape(32, 16, 128)
    part = lax.all_to_all(copies, ("yh", "ta"), 0, 0, tiled=True).reshape(512, 128)
    plane = exchange(part, 8, ("x", "yl")).reshape(4, 2, 4, 128, 128)
    own = jnp.transpose(plane, (0, 2, 1, 3, 4)).reshape(32, 128, 128)
    other = lax.ppermute(own, "c", [(0, 1), (1, 0)])
    core = lax.axis_index("c")
    top = jnp.maximum(jnp.max(jnp.abs(own), axis=(0, 1)), jnp.max(jnp.abs(other), axis=(0, 1)))
    channel_scale = top.astype(jnp.float32)
    first = jnp.where(core == 0, own, other)
    second = jnp.where(core == 0, other, own)
    weight = jnp.stack([first, second], 1).astype(jnp.float32)
    serving_weight = (weight / channel_scale).astype(jnp.bfloat16)
    return serving_weight.reshape(LAYERS, D, HEAD), channel_scale[None]


def solution(mesh):
    fine = Mesh(mesh.devices.reshape(4, 4, 2, 2, 8), AXES)
    out_specs = (P(None, None, "ta"), P(None, "ta"))
    return jax.shard_map(shards, mesh=fine, in_specs=(P(AXES),), out_specs=out_specs, check_vma=False)
```

time: 118 us -> 58.1 us (0.49)
  waiting for transfers between devices: 81 us -> 2.1 us
  blocking collectives: 17.5 us -> 45.5 us
  between operations: 14 us -> 0.7 us
  starting transfers between devices: 0.04 us -> 5.11 us
    all_gather x1 -> x0, waiting for transfers between devices: 81 us -> none  [relayout(): complete = lax.all_gather(regrouped, 'gx', axis=0, tiled=True)]
    all_to_all x1 -> x2, blocking collectives: 17.5 us -> 45.5 us  [the longest x1 28.2 us: shards(): lax.all_to_all(copies, ('yh', 'ta'), 0, 0, tiled=True).reshape(512, 128)]
    ppermute x0 -> x1, starting transfers between devices: none -> 5.11 us  [shards(): other = lax.ppermute(own, 'c', [(0, 1), (1, 0)])]
    ppermute x0 -> x1, waiting for transfers between devices: none -> 2.1 us  [shards(): other = lax.ppermute(own, 'c', [(0, 1), (1, 0)])]
    reduce_max x1, other arithmetic: 2.03 us -> 0.16 us  [shards(): jnp.max(jnp.abs(own), axis=(0, 1))]
    convert_element_type x2 -> x3, other arithmetic: 2.57 us -> 1.95 us  [the longest x1 1.66 us: shards(): serving_weight = (weight / channel_scale).astype(jnp.bfloat16)]
where the time goes in v1:
time: 58.1 us; the launch traced here: 57.9 us
  blocking collectives  45.5 us (78%)
  starting transfers between devices  5.11 us (9%)
  other arithmetic  3.73 us (6%)
  waiting for transfers between devices  2.1 us (4%)
  local copies, waits for them, and re-layouts  0.76 us (1%)
  between operations  0.7 us (1%)
    all_to_all x1, blocking collectives, shards(): lax.all_to_all(copies, ('yh', 'ta'), 0, 0, tiled=True).reshape(512, 128)  28.2 us
    all_to_all x1, blocking collectives, exchange(): return lax.all_to_all(copies, axes, 0, 0, tiled=True)  17.3 us
    ppermute x1, starting transfers between devices, shards(): other = lax.ppermute(own, 'c', [(0, 1), (1, 0)])  5.11 us
    ppermute x1, waiting for transfers between devices, shards(): other = lax.ppermute(own, 'c', [(0, 1), (1, 0)])  2.1 us
    convert_element_type x1, other arithmetic, shards(): serving_weight = (weight / channel_scale).astype(jnp.bfloat16)  1.66 us
  transfers between devices with their start and end apart: 1, of which 1 were waited for; matrix products, arithmetic and copies ran while one was open for 0% of the time, Pallas kernels for 0%

profile of v1, /device:TPU:1, one launch (start us, length us, event | category | flops | bytes accessed | tf_op | source)
XLA Modules:
  0.0 57.9 jit_solution(677348076549326020)
XLA Ops:
  0.6 0.8 %convert_bitcast_fusion = bf16[8,16,128]{2,0,1:T(8,128)(2,1)S(1)} fusion(f32[16384]{0:T(1024)} %param.1), kind=kLoop, calls=%fused_computation.6 | loop fusion | flops 16384 | bytes 98304 | tf_op jit(solution)/shard_map/transpose | solution.py:20
  1.5 28.2 %all_to_all.10 = bf16[32,16,128]{2,1,0:T(8,128)(2,1)S(1)} all-to-all(bf16[32,16,128]{2,1,0:T(8,128)(2,1)S(1)} %bitcast.23), channel_id=1, replica_groups=mesh['x'=4,'yh'=4,'yl'=2,'c'=2,'ta'=8] {'yh','ta'}, dimensions={0} | all-to-all | bytes 262144 | tf_op jit(solution)/shard_map/all_to_all | solution.py:22
  29.7 0.1 broadcast_in_dim.8
  29.9 17.3 %all_to_all.11 = bf16[8,512,128]{2,1,0:T(8,128)(2,1)S(1)} all-to-all(bf16[8,512,128]{2,1,0:T(8,128)(2,1)S(1)} %broadcast_in_dim.8), channel_id=1, replica_groups=mesh['x'=4,'yh'=4,'yl'=2,'c'=2,'ta'=8] {'x','yl'}, dimensions={0} | all-to-all | bytes 2097152 | tf_op jit(solution)/shard_map/all_to_all | solution.py:15
  47.2 0.1 copy.9
  47.3 5.1 %collective-permute-start = (bf16[32,128,128]{2,1,0:T(8,128)(2,1)S(1)}, bf16[32,128,128]{2,1,0:T(8,128)(2,1)S(1)}, u32[]{:S(2)}, u32[]{:S(2)}) collective-permute-start(bf16[32,128,128]{2,1,0:T(8,128)(2,1)S(1)} %bitcast.21), channel_id=1, source_target_pairs={{0,8},{8,0},{1,9},{9,1},{2,10},{10,2},{3,11},{11,3},{4,12},{12,4},... | collective-permute-start | bytes 3145736 | tf_op jit(solution)/shard_map/ppermute | solution.py:25
  52.4 0.2 abs_reduce_fusion.1
  52.5 2.1 %collective-permute-done = bf16[32,128,128]{2,1,0:T(8,128)(2,1)S(1)} collective-permute-done((bf16[32,128,128]{2,1,0:T(8,128)(2,1)S(1)}, bf16[32,128,128]{2,1,0:T(8,128)(2,1)S(1)}, u32[]{:S(2)}, u32[]{:S(2)}) %collective-permute-start) | collective-permute-done | bytes 1048608 | tf_op jit(solution)/shard_map/ppermute | solution.py:25
  54.6 0.8 %select_bitcast_fusion.1 = (bf16[32,1,128,128]{3,2,0,1:T(8,128)(2,1)S(1)}, bf16[32,1,128,128]{3,2,0,1:T(8,128)(2,1)S(1)}, bf16[128]{0:T(256)(128)(2,1)S(1)}) fusion(bf16[32,128,128]{2,1,0:T(8,128)(2,1)S(1)} %collective-permute-done, pred[]{:T(512)S(6)} %eq.4, bf16[4,4,2,128,128]{4,3,2,1,0:T(8,128)(2,1)S(1)} %copy.9), kind=kLoop, calls=%fused_computation.5 | loop fusion | flops 2097024 | bytes 4194561 | tf_op jit(solution)/shard_map/stack | solution.py:31
  55.4 0.3 maximum_convert_fusion
  55.7 0.5 copy.10
  56.2 0.0 copy-start
  56.2 1.7 %divide_convert_fusion = bf16[1,8192,128]{2,1,0:T(8,128)(2,1)} fusion(f32[1,8192,128]{2,1,0:T(8,128)S(1)} %bitcast.18, f32[128]{0:T(128)S(1)} %maximum_convert_fusion.1), kind=kLoop, calls=%fused_computation | loop fusion | flops 2097152 | bytes 6291968 | tf_op jit(solution)/shard_map/convert_element_type | solution.py:32
  57.9 0.0 copy-done
  (3 shorter events, 0.0 us)
Async XLA Ops:
  47.3 7.4 %collective-permute-start = (bf16[32,128,128]{2,1,0:T(8,128)(2,1)S(1)}, bf16[32,128,128]{2,1,0:T(8,128)(2,1)S(1)}, u32[]{:S(2)}, u32[]{:S(2)}) collective-permute-start(bf16[32,128,128]{2,1,0:T(8,128)(2,1)S(1)} %bitcast.21), channel_id=1, source_target_pairs={{0,8},{8,0},{1,9},{9,1},{2,10},{10,2},{3,11},{11,3},{4,12},{12,4},... | collective-permute-start | bytes 3145736 | tf_op jit(solution)/shard_map/ppermute | solution.py:25
  56.2 1.7 %copy-start = (f32[128]{0:T(128)}, f32[128]{0:T(128)S(1)}, u32[]{:S(2)}) copy-start(f32[128]{0:T(128)S(1)} %maximum_convert_fusion.1) | copy-start | bytes 1540

commit v2 on v1

v2 whole, which is shorter than its diff:
```python
import jax
import jax.numpy as jnp
from jax import lax
from jax.experimental import pallas as pl
from jax.experimental.pallas import tpu as pltpu
from jax.sharding import Mesh, PartitionSpec as P

D = 8192
KVH = 8
HEAD = 128
LAYERS = 1
X, Y, C, Z = 4, 8, 2, 8
AXES = ("x", "y", "c", "ta")
ROWS = 128


def device(x, y, c, z):
    return (((x % X) * Y + y % Y) * C + c) * Z + z


def far_groups():
    return [
        [device(x, 2 * yh + yp, c, z) for yh in range(Y // 2) for z in range(Z)]
        for x in range(X) for yp in range(2) for c in range(C)
    ]


def near_groups():
    return [
        [device(x, y, c, z) for x in range(X) for y in (2 * j, 2 * j + 1)]
        for c in range(C) for z in range(Z) for j in range(Y // 2)
    ]


def exchange(blocks, groups):
    return lax.all_to_all(blocks, AXES, 0, 0, axis_index_groups=groups, tiled=True)


CHUNKS = 8


def finish_kernel(top_ref, own_ref, other_ref, out_ref, scale_ref, stage_ref, row_ref, sems):
    core = lax.axis_index("c")
    top = jnp.maximum(top_ref[...], jnp.max(jnp.abs(other_ref[...]).reshape(-1, 16, HEAD), axis=0).max(axis=0, keepdims=True))
    scale = top.astype(jnp.float32)
    row_ref[...] = scale
    factor = 1.0 / scale
    copies = [pltpu.make_async_copy(row_ref, scale_ref, sems.at[CHUNKS])]
    copies[0].start()
    for k in range(CHUNKS):
        x, part = divmod(k, 2)
        for yh in (2 * part, 2 * part + 1):
            for yp in range(2):
                source = (x * 2 + yp) * 4 + yh
                target = (x * 4 + yh) * 2 + yp
                stage_ref[target, core] = (own_ref[source].astype(jnp.float32) * factor).astype(jnp.bfloat16)
                stage_ref[target, 1 - core] = (other_ref[source].astype(jnp.float32) * factor).astype(jnp.bfloat16)
        copy = pltpu.make_async_copy(stage_ref.at[pl.ds(4 * k, 4)], out_ref.at[pl.ds(4 * k, 4)], sems.at[k])
        copy.start()
        copies.append(copy)
    for copy in copies:
        copy.wait()


def finish(top, own, other):
    vmem = pl.BlockSpec(memory_space=pltpu.VMEM)
    return pl.pallas_call(
        finish_kernel,
        in_specs=[vmem, vmem, vmem],
        out_specs=[pl.BlockSpec(memory_space=pl.ANY), pl.BlockSpec(memory_space=pl.ANY)],
        out_shape=[
            jax.ShapeDtypeStruct((32, 2, ROWS, HEAD), jnp.bfloat16),
            jax.ShapeDtypeStruct((1, HEAD), jnp.float32),
        ],
        scratch_shapes=[
            pltpu.VMEM((32, 2, ROWS, HEAD), jnp.bfloat16),
            pltpu.VMEM((1, HEAD), jnp.float32),
            pltpu.SemaphoreType.DMA((CHUNKS + 1,)),
        ],
        name="finish",
    )(*(pltpu.with_memory_space_constraint(part, pltpu.VMEM) for part in (top, own, other)))


def shards(master_flat):
    rounded = master_flat.astype(jnp.bfloat16).reshape(16, 8, HEAD)
    by_channel = jnp.transpose(rounded, (1, 0, 2))
    copies = jnp.broadcast_to(by_channel[None], (4, 8, 16, HEAD)).reshape(32, 16, HEAD)
    far = exchange(copies, far_groups()).reshape(512, HEAD)
    copies = jnp.broadcast_to(far[None], (8, 512, HEAD))
    own = exchange(copies, near_groups()).reshape(32, ROWS, HEAD)
    other = lax.ppermute(own, "c", [(0, 1), (1, 0)])
    top = jnp.max(jnp.abs(own), axis=(0, 1))[None]
    weight, channel_scale = finish(top, own, other)
    return weight.reshape(LAYERS, D, HEAD), channel_scale


def solution(mesh):
    fine = Mesh(mesh.devices.reshape(X, Y, C, Z), AXES)
    out_specs = (P(None, None, "ta"), P(None, "ta"))
    return jax.shard_map(shards, mesh=fine, in_specs=(P(AXES),), out_specs=out_specs, check_vma=False)
```

time: 58.1 us -> 56.6 us (0.974)
  other arithmetic: 3.73 us -> 1 us
  Pallas kernels: 0 us -> 1.81 us
  local copies, waits for them, and re-layouts: 0.76 us -> 0.16 us
    convert_element_type x3 -> x0, other arithmetic: 1.95 us -> none  [the longest x1 1.66 us: shards(): serving_weight = (weight / channel_scale).astype(jnp.bfloat16)]
    pallas_call x0 -> x1, Pallas kernels: none -> 1.81 us  [finish(): pl.pallas_call(finish_kernel, in_specs=[vmem, vmem, vmem], out_specs=[pl....]
    another operation x1 -> x0, other arithmetic: 0.78 us -> none  [shards(): weight = jnp.stack([first, second], 1).astype(jnp.float32)]
where the time goes in v2:
time: 56.6 us; the launch traced here: 56.3 us
  blocking collectives  45.5 us (80%)
  starting transfers between devices  5.1 us (9%)
  waiting for transfers between devices  2.11 us (4%)
  Pallas kernels  1.81 us (3%)
  other arithmetic  1 us (2%)
  between operations  0.65 us (1%)
    all_to_all x2, blocking collectives, exchange(): lax.all_to_all(blocks, AXES, 0, 0, axis_index_groups=groups, tiled=True)  45.5 us
    ppermute x1, starting transfers between devices, shards(): other = lax.ppermute(own, 'c', [(0, 1), (1, 0)])  5.1 us
    ppermute x1, waiting for transfers between devices, shards(): other = lax.ppermute(own, 'c', [(0, 1), (1, 0)])  2.11 us
    pallas_call x1, Pallas kernels, finish(): pl.pallas_call(finish_kernel, in_specs=[vmem, vmem, vmem], out_specs=[pl....  1.81 us
  transfers between devices with their start and end apart: 1, of which 1 were waited for; matrix products, arithmetic and copies ran while one was open for 0% of the time, Pallas kernels for 0%

profile of v2, /device:TPU:1, one launch (start us, length us, event | category | flops | bytes accessed | tf_op | source)
XLA Modules:
  0.0 56.3 jit_solution(4935620822891201801)
XLA Ops:
  0.6 0.8 %convert_bitcast_fusion = bf16[8,16,128]{2,0,1:T(8,128)(2,1)S(1)} fusion(f32[16384]{0:T(1024)} %param.1), kind=kLoop, calls=%fused_computation.1 | loop fusion | flops 16384 | bytes 98304 | tf_op jit(solution)/shard_map/transpose | solution.py:86
  1.5 28.2 %all_to_all.10 = bf16[32,16,128]{2,1,0:T(8,128)(2,1)S(1)} all-to-all(bf16[32,16,128]{2,1,0:T(8,128)(2,1)S(1)} %bitcast.13), channel_id=1, replica_groups={{0,1,2,3,4,5,6,7,32,33,34,35,36,37,38,39,64,65,66,67,68,69,70,71,96,97,..., dimensions={0} | all-to-all | bytes 262144 | tf_op jit(solution)/shard_map/all_to_all | solution.py:36
  29.7 0.1 broadcast_in_dim.18
  29.9 17.3 %all_to_all.11 = bf16[8,512,128]{2,1,0:T(8,128)(2,1)S(1)} all-to-all(bf16[8,512,128]{2,1,0:T(8,128)(2,1)S(1)} %broadcast_in_dim.18), channel_id=1, replica_groups={{0,16,128,144,256,272,384,400},{32,48,160,176,288,304,416,432},{64,80,1..., dimensions={0} | all-to-all | bytes 2097152 | tf_op jit(solution)/shard_map/all_to_all | solution.py:36
  47.2 5.1 %collective-permute-start = (bf16[32,128,128]{2,1,0:T(8,128)(2,1)S(1)}, bf16[32,128,128]{2,1,0:T(8,128)(2,1)S(1)}, u32[]{:S(2)}, u32[]{:S(2)}) collective-permute-start(bf16[32,128,128]{2,1,0:T(8,128)(2,1)S(1)} %bitcast.9), channel_id=1, source_target_pairs={{0,8},{8,0},{1,9},{9,1},{2,10},{10,2},{3,11},{11,3},{4,12},{12,4},... | collective-permute-start | bytes 3145736 | tf_op jit(solution)/shard_map/ppermute | solution.py:91
  52.3 0.2 abs_reduce_fusion
  52.4 2.1 %collective-permute-done.other_ref = bf16[32,128,128]{2,1,0:T(8,128)(2,1)S(1)} collective-permute-done((bf16[32,128,128]{2,1,0:T(8,128)(2,1)S(1)}, bf16[32,128,128]{2,1,0:T(8,128)(2,1)S(1)}, u32[]{:S(2)}, u32[]{:S(2)}) %collective-permute-start) | collective-permute-done | bytes 1048608 | tf_op jit(solution)/shard_map/ppermute | solution.py:91
  54.5 1.8 %finish.1 = (bf16[32,2,128,128]{3,2,1,0:T(8,128)(2,1)}, f32[1,128]{1,0:T(1,128)}) custom-call(bf16[1,128]{1,0:T(2,128)(2,1)S(1)} %bitcast.11, bf16[32,128,128]{2,1,0:T(8,128)(2,1)S(1)} %bitcast.10, bf16[32,128,128]{2,1,0:T(8,128)(2,1)S(1)} %collective-permute-done.other_ref), custom_call_target="tpu_custom_call" | custom-call | tf_op jit(solution)/shard_map/finish/pallas_call | solution.py:67
  (2 shorter events, 0.0 us)
Async XLA Ops:
  47.2 7.4 %collective-permute-start = (bf16[32,128,128]{2,1,0:T(8,128)(2,1)S(1)}, bf16[32,128,128]{2,1,0:T(8,128)(2,1)S(1)}, u32[]{:S(2)}, u32[]{:S(2)}) collective-permute-start(bf16[32,128,128]{2,1,0:T(8,128)(2,1)S(1)} %bitcast.9), channel_id=1, source_target_pairs={{0,8},{8,0},{1,9},{9,1},{2,10},{10,2},{3,11},{11,3},{4,12},{12,4},... | collective-permute-start | bytes 3145736 | tf_op jit(solution)/shard_map/ppermute | solution.py:91

commit v3 on v2

--- a/solution.py
+++ b/solution.py
@@ -20,15 +20,19 @@
 
 def far_groups():
     return [
-        [device(x, 2 * yh + yp, c, z) for yh in range(Y // 2) for z in range(Z)]
-        for x in range(X) for yp in range(2) for c in range(C)
+        [device(x, 2 * yh + yp, c, 2 * zh + zp) for yh in range(Y // 2) for zh in range(Z // 2)]
+        for x in range(X) for yp in range(2) for c in range(C) for zp in range(2)
     ]
+
+
+def pairs(size, c):
+    return [(2 * i, (2 * i + 1 - 2 * c) % size) for i in range(size // 2)]
 
 
 def near_groups():
     return [
-        [device(x, y, c, z) for x in range(X) for y in (2 * j, 2 * j + 1)]
-        for c in range(C) for z in range(Z) for j in range(Y // 2)
+        [device(x, y, c, z) for x in range(X) for y in ys for z in zs]
+        for c in range(C) for ys in pairs(Y, c) for zs in pairs(Z, c)
     ]
 
 
@@ -51,10 +55,11 @@
         x, part = divmod(k, 2)
         for yh in (2 * part, 2 * part + 1):
             for yp in range(2):
-                source = (x * 2 + yp) * 4 + yh
                 target = (x * 4 + yh) * 2 + yp
-                stage_ref[target, core] = (own_ref[source].astype(jnp.float32) * factor).astype(jnp.bfloat16)
-                stage_ref[target, 1 - core] = (other_ref[source].astype(jnp.float32) * factor).astype(jnp.bfloat16)
+                for zp in range(2):
+                    source = ((x * 2 + yp) * 2 + zp) * 4 + yh
+                    stage_ref[target, core, :, zp] = (own_ref[source].astype(jnp.float32) * factor).astype(jnp.bfloat16)
+                    stage_ref[target, 1 - core, :, zp] = (other_ref[source].astype(jnp.float32) * factor).astype(jnp.bfloat16)
         copy = pltpu.make_async_copy(stage_ref.at[pl.ds(4 * k, 4)], out_ref.at[pl.ds(4 * k, 4)], sems.at[k])
         copy.start()
         copies.append(copy)
@@ -69,11 +74,11 @@
         in_specs=[vmem, vmem, vmem],
         out_specs=[pl.BlockSpec(memory_space=pl.ANY), pl.BlockSpec(memory_space=pl.ANY)],
         out_shape=[
-            jax.ShapeDtypeStruct((32, 2, ROWS, HEAD), jnp.bfloat16),
+            jax.ShapeDtypeStruct((32, 2, Z // 2, 2, 16, HEAD), jnp.bfloat16),
             jax.ShapeDtypeStruct((1, HEAD), jnp.float32),
         ],
         scratch_shapes=[
-            pltpu.VMEM((32, 2, ROWS, HEAD), jnp.bfloat16),
+            pltpu.VMEM((32, 2, Z // 2, 2, 16, HEAD), jnp.bfloat16),
             pltpu.VMEM((1, HEAD), jnp.float32),
             pltpu.SemaphoreType.DMA((CHUNKS + 1,)),
         ],
@@ -84,12 +89,18 @@
 def shards(master_flat):
     rounded = master_flat.astype(jnp.bfloat16).reshape(16, 8, HEAD)
     by_channel = jnp.transpose(rounded, (1, 0, 2))
-    copies = jnp.broadcast_to(by_channel[None], (4, 8, 16, HEAD)).reshape(32, 16, HEAD)
-    far = exchange(copies, far_groups()).reshape(512, HEAD)
-    copies = jnp.broadcast_to(far[None], (8, 512, HEAD))
-    own = exchange(copies, near_groups()).reshape(32, ROWS, HEAD)
+    even, odd = by_channel[0::2], by_channel[1::2]
+    second_core, odd_plane = lax.axis_index("c") == 1, lax.axis_index("ta") % 2 == 1
+    even = jnp.where(second_core & odd_plane, jnp.roll(even, -1, 0), even)
+    odd = jnp.where(second_core & ~odd_plane, jnp.roll(odd, 1, 0), odd)
+    by_pair = jnp.stack([even, odd], 1)
+    copies = jnp.broadcast_to(by_pair[None], (4, 4, 2, 16, HEAD)).reshape(16, 2, 16, HEAD)
+    far = exchange(copies, far_groups())
+    far = jnp.transpose(far, (1, 0, 2, 3))
+    copies = jnp.broadcast_to(far[None], (8, 2, 16, 16, HEAD)).reshape(16, 16, 16, HEAD)
+    own = exchange(copies, near_groups()).reshape(64, 4, 16, HEAD)
     other = lax.ppermute(own, "c", [(0, 1), (1, 0)])
-    top = jnp.max(jnp.abs(own), axis=(0, 1))[None]
+    top = jnp.max(jnp.abs(own), axis=(0, 1, 2))[None]
     weight, channel_scale = finish(top, own, other)
     return weight.reshape(LAYERS, D, HEAD), channel_scale
 

time: 56.6 us -> 55.9 us (0.988)
  starting transfers between devices: 5.1 us -> 3.97 us
    ppermute x1, starting transfers between devices: 5.1 us -> 3.97 us  [shards(): other = lax.ppermute(own, 'c', [(0, 1), (1, 0)])]
where the time goes in v3:
time: 55.9 us; the launch traced here: 55.6 us
  blocking collectives  45.6 us (82%)
  starting transfers between devices  3.97 us (7%)
  waiting for transfers between devices  2.11 us (4%)
  Pallas kernels  1.81 us (3%)
  other arithmetic  1.09 us (2%)
  between operations  0.73 us (1%)
    all_to_all x2, blocking collectives, exchange(): lax.all_to_all(blocks, AXES, 0, 0, axis_index_groups=groups, tiled=True)  45.6 us
    ppermute x1, starting transfers between devices, shards(): other = lax.ppermute(own, 'c', [(0, 1), (1, 0)])  3.97 us
    ppermute x1, waiting for transfers between devices, shards(): other = lax.ppermute(own, 'c', [(0, 1), (1, 0)])  2.11 us
    pallas_call x1, Pallas kernels, finish(): pl.pallas_call(finish_kernel, in_specs=[vmem, vmem, vmem], out_specs=[pl....  1.81 us
  transfers between devices with their start and end apart: 1, of which 1 were waited for; matrix products, arithmetic and copies ran while one was open for 0% of the time, Pallas kernels for 0%

profile of v3, /device:TPU:1, one launch (start us, length us, event | category | flops | bytes accessed | tf_op | source)
XLA Modules:
  0.0 55.6 jit_solution(2453723233814949853)
XLA Ops:
  0.6 0.8 %convert_bitcast_fusion = bf16[8,16,128]{2,0,1:T(8,128)(2,1)S(1)} fusion(f32[16384]{0:T(1024)} %param.1), kind=kLoop, calls=%fused_computation.2 | loop fusion | flops 16384 | bytes 98304 | tf_op jit(solution)/shard_map/transpose | solution.py:91
  1.6 0.1 fusion
  1.8 27.7 %all_to_all.10 = bf16[16,2,16,128]{3,2,1,0:T(8,128)(2,1)S(1)} all-to-all(bf16[16,2,16,128]{3,2,1,0:T(8,128)(2,1)S(1)} %bitcast.19), channel_id=1, replica_groups={{0,2,4,6,32,34,36,38,64,66,68,70,96,98,100,102},{1,3,5,7,33,35,37,39,65..., dimensions={0} | all-to-all | bytes 262144 | tf_op jit(solution)/shard_map/all_to_all | solution.py:40
  29.5 0.2 broadcast_in_dim.7
  29.7 17.9 %all_to_all.11 = bf16[16,16,16,128]{3,2,1,0:T(8,128)(2,1)S(1)} all-to-all(bf16[16,16,16,128]{3,2,1,0:T(8,128)(2,1)S(1)} %bitcast.18), channel_id=1, replica_groups={{0,1,16,17,128,129,144,145,256,257,272,273,384,385,400,401},{2,3,18,19,..., dimensions={0} | all-to-all | bytes 2097152 | tf_op jit(solution)/shard_map/all_to_all | solution.py:40
  47.6 4.0 %collective-permute-start = (bf16[64,4,16,128]{3,2,1,0:T(8,128)(2,1)S(1)}, bf16[64,4,16,128]{3,2,1,0:T(8,128)(2,1)S(1)}, u32[]{:S(2)}, u32[]{:S(2)}) collective-permute-start(bf16[64,4,16,128]{3,2,1,0:T(8,128)(2,1)S(1)} %bitcast.15), channel_id=1, source_target_pairs={{0,8},{8,0},{1,9},{9,1},{2,10},{10,2},{3,11},{11,3},{4,12},{12,4},... | collective-permute-start | bytes 3145736 | tf_op jit(solution)/shard_map/ppermute | solution.py:102
  51.6 0.2 abs_reduce_fusion
  51.7 2.1 %collective-permute-done.other_ref = bf16[64,4,16,128]{3,2,1,0:T(8,128)(2,1)S(1)} collective-permute-done((bf16[64,4,16,128]{3,2,1,0:T(8,128)(2,1)S(1)}, bf16[64,4,16,128]{3,2,1,0:T(8,128)(2,1)S(1)}, u32[]{:S(2)}, u32[]{:S(2)}) %collective-permute-start) | collective-permute-done | bytes 1048608 | tf_op jit(solution)/shard_map/ppermute | solution.py:102
  53.8 1.8 %finish.1 = (bf16[32,2,4,2,16,128]{5,4,3,2,1,0:T(8,128)(2,1)}, f32[1,128]{1,0:T(1,128)}) custom-call(bf16[1,128]{1,0:T(2,128)(2,1)S(1)} %bitcast.17, bf16[64,4,16,128]{3,2,1,0:T(8,128)(2,1)S(1)} %bitcast.16, bf16[64,4,16,128]{3,2,1,0:T(8,128)(2,1)S(1)} %collective-permute-done.other_ref), custom_call_target="tpu_custom_call" | custom-call | tf_op jit(solution)/shard_map/finish/pallas_call | solution.py:72
  (9 shorter events, 0.2 us)
Async XLA Ops:
  47.6 6.2 %collective-permute-start = (bf16[64,4,16,128]{3,2,1,0:T(8,128)(2,1)S(1)}, bf16[64,4,16,128]{3,2,1,0:T(8,128)(2,1)S(1)}, u32[]{:S(2)}, u32[]{:S(2)}) collective-permute-start(bf16[64,4,16,128]{3,2,1,0:T(8,128)(2,1)S(1)} %bitcast.15), channel_id=1, source_target_pairs={{0,8},{8,0},{1,9},{9,1},{2,10},{10,2},{3,11},{11,3},{4,12},{12,4},... | collective-permute-start | bytes 3145736 | tf_op jit(solution)/shard_map/ppermute | solution.py:102

commit v4 on v3

--- a/solution.py
+++ b/solution.py
@@ -32,7 +32,7 @@
 def near_groups():
     return [
         [device(x, y, c, z) for x in range(X) for y in ys for z in zs]
-        for c in range(C) for ys in pairs(Y, c) for zs in pairs(Z, c)
+        for c in range(C) for ys in pairs(Y, c) for zs in pairs(Z, 0)
     ]
 
 
@@ -89,11 +89,7 @@
 def shards(master_flat):
     rounded = master_flat.astype(jnp.bfloat16).reshape(16, 8, HEAD)
     by_channel = jnp.transpose(rounded, (1, 0, 2))
-    even, odd = by_channel[0::2], by_channel[1::2]
-    second_core, odd_plane = lax.axis_index("c") == 1, lax.axis_index("ta") % 2 == 1
-    even = jnp.where(second_core & odd_plane, jnp.roll(even, -1, 0), even)
-    odd = jnp.where(second_core & ~odd_plane, jnp.roll(odd, 1, 0), odd)
-    by_pair = jnp.stack([even, odd], 1)
+    by_pair = by_channel.reshape(4, 2, 16, HEAD)
     copies = jnp.broadcast_to(by_pair[None], (4, 4, 2, 16, HEAD)).reshape(16, 2, 16, HEAD)
     far = exchange(copies, far_groups())
     far = jnp.transpose(far, (1, 0, 2, 3))

time: 55.9 us -> 56.6 us (1.013)
  starting transfers between devices: 3.97 us -> 6.4 us
  blocking collectives: 45.6 us -> 44.2 us
    ppermute x1, starting transfers between devices: 3.97 us -> 6.4 us  [shards(): other = lax.ppermute(own, 'c', [(0, 1), (1, 0)])]
    all_to_all x2, blocking collectives: 45.6 us -> 44.2 us  [exchange(): lax.all_to_all(blocks, AXES, 0, 0, axis_index_groups=groups, tiled=True)]
where the time goes in v4:
time: 56.6 us; the launch traced here: 56.4 us
  blocking collectives  44.2 us (78%)
  starting transfers between devices  6.4 us (11%)
  waiting for transfers between devices  2.11 us (4%)
  Pallas kernels  1.81 us (3%)
  other arithmetic  1 us (2%)
  between operations  0.66 us (1%)
    all_to_all x2, blocking collectives, exchange(): lax.all_to_all(blocks, AXES, 0, 0, axis_index_groups=groups, tiled=True)  44.2 us
    ppermute x1, starting transfers between devices, shards(): other = lax.ppermute(own, 'c', [(0, 1), (1, 0)])  6.4 us
    ppermute x1, waiting for transfers between devices, shards(): other = lax.ppermute(own, 'c', [(0, 1), (1, 0)])  2.11 us
    pallas_call x1, Pallas kernels, finish(): pl.pallas_call(finish_kernel, in_specs=[vmem, vmem, vmem], out_specs=[pl....  1.81 us
  transfers between devices with their start and end apart: 1, of which 1 were waited for; matrix products, arithmetic and copies ran while one was open for 0% of the time, Pallas kernels for 0%

profile of v4, /device:TPU:1, one launch (start us, length us, event | category | flops | bytes accessed | tf_op | source)
XLA Modules:
  0.0 56.4 jit_solution(608453423176465048)
XLA Ops:
  0.6 0.8 %convert_bitcast_fusion = bf16[8,16,128]{2,0,1:T(8,128)(2,1)S(1)} fusion(f32[16384]{0:T(1024)} %param.1), kind=kLoop, calls=%fused_computation.1 | loop fusion | flops 16384 | bytes 98304 | tf_op jit(solution)/shard_map/transpose | solution.py:91
  1.5 27.7 %all_to_all.10 = bf16[16,2,16,128]{3,2,1,0:T(8,128)(2,1)S(1)} all-to-all(bf16[16,2,16,128]{3,2,1,0:T(8,128)(2,1)S(1)} %bitcast.15), channel_id=1, replica_groups={{0,2,4,6,32,34,36,38,64,66,68,70,96,98,100,102},{1,3,5,7,33,35,37,39,65..., dimensions={0} | all-to-all | bytes 262144 | tf_op jit(solution)/shard_map/all_to_all | solution.py:40
  29.2 0.2 broadcast_in_dim.18
  29.5 16.4 %all_to_all.11 = bf16[16,16,16,128]{3,2,1,0:T(8,128)(2,1)S(1)} all-to-all(bf16[16,16,16,128]{3,2,1,0:T(8,128)(2,1)S(1)} %bitcast.14), channel_id=1, replica_groups={{0,1,16,17,128,129,144,145,256,257,272,273,384,385,400,401},{2,3,18,19,..., dimensions={0} | all-to-all | bytes 2097152 | tf_op jit(solution)/shard_map/all_to_all | solution.py:40
  45.9 6.4 %collective-permute-start = (bf16[64,4,16,128]{3,2,1,0:T(8,128)(2,1)S(1)}, bf16[64,4,16,128]{3,2,1,0:T(8,128)(2,1)S(1)}, u32[]{:S(2)}, u32[]{:S(2)}) collective-permute-start(bf16[64,4,16,128]{3,2,1,0:T(8,128)(2,1)S(1)} %bitcast.11), channel_id=1, source_target_pairs={{0,8},{8,0},{1,9},{9,1},{2,10},{10,2},{3,11},{11,3},{4,12},{12,4},... | collective-permute-start | bytes 3145736 | tf_op jit(solution)/shard_map/ppermute | solution.py:98
  52.3 0.2 abs_reduce_fusion
  52.5 2.1 %collective-permute-done.other_ref = bf16[64,4,16,128]{3,2,1,0:T(8,128)(2,1)S(1)} collective-permute-done((bf16[64,4,16,128]{3,2,1,0:T(8,128)(2,1)S(1)}, bf16[64,4,16,128]{3,2,1,0:T(8,128)(2,1)S(1)}, u32[]{:S(2)}, u32[]{:S(2)}) %collective-permute-start) | collective-permute-done | bytes 1048608 | tf_op jit(solution)/shard_map/ppermute | solution.py:98
  54.6 1.8 %finish.1 = (bf16[32,2,4,2,16,128]{5,4,3,2,1,0:T(8,128)(2,1)}, f32[1,128]{1,0:T(1,128)}) custom-call(bf16[1,128]{1,0:T(2,128)(2,1)S(1)} %bitcast.13, bf16[64,4,16,128]{3,2,1,0:T(8,128)(2,1)S(1)} %bitcast.12, bf16[64,4,16,128]{3,2,1,0:T(8,128)(2,1)S(1)} %collective-permute-done.other_ref), custom_call_target="tpu_custom_call" | custom-call | tf_op jit(solution)/shard_map/finish/pallas_call | solution.py:72
  (3 shorter events, 0.0 us)
Async XLA Ops:
  45.9 8.7 %collective-permute-start = (bf16[64,4,16,128]{3,2,1,0:T(8,128)(2,1)S(1)}, bf16[64,4,16,128]{3,2,1,0:T(8,128)(2,1)S(1)}, u32[]{:S(2)}, u32[]{:S(2)}) collective-permute-start(bf16[64,4,16,128]{3,2,1,0:T(8,128)(2,1)S(1)} %bitcast.11), channel_id=1, source_target_pairs={{0,8},{8,0},{1,9},{9,1},{2,10},{10,2},{3,11},{11,3},{4,12},{12,4},... | collective-permute-start | bytes 3145736 | tf_op jit(solution)/shard_map/ppermute | solution.py:98

commit v5 on v4

--- a/solution.py
+++ b/solution.py
@@ -32,7 +32,7 @@
 def near_groups():
     return [
         [device(x, y, c, z) for x in range(X) for y in ys for z in zs]
-        for c in range(C) for ys in pairs(Y, c) for zs in pairs(Z, 0)
+        for c in range(C) for ys in pairs(Y, c) for zs in pairs(Z, c)
     ]
 
 
@@ -86,11 +86,30 @@
     )(*(pltpu.with_memory_space_constraint(part, pltpu.VMEM) for part in (top, own, other)))
 
 
+def spread_kernel(flat_ref, out_ref):
+    second_core, odd_plane = lax.axis_index("c"), lax.axis_index("ta") % 2
+    for zh in range(Z // 2):
+        even = (2 * zh + 2 * second_core * odd_plane) % Z
+        odd = (2 * zh + 1 + (Z - 2) * second_core * (1 - odd_plane)) % Z
+        for zl, channel in enumerate((even, odd)):
+            block = flat_ref[pl.ds(channel, 16, stride=Z), :].astype(jnp.bfloat16)
+            for yh in range(Y // 2):
+                out_ref[yh * 4 + zh, zl] = block
+
+
+def spread(flat):
+    vmem = pl.BlockSpec(memory_space=pltpu.VMEM)
+    return pl.pallas_call(
+        spread_kernel,
+        in_specs=[vmem],
+        out_specs=vmem,
+        out_shape=pltpu.VMEM((16, 2, 16, HEAD), jnp.bfloat16),
+        name="spread",
+    )(flat)
+
+
 def shards(master_flat):
-    rounded = master_flat.astype(jnp.bfloat16).reshape(16, 8, HEAD)
-    by_channel = jnp.transpose(rounded, (1, 0, 2))
-    by_pair = by_channel.reshape(4, 2, 16, HEAD)
-    copies = jnp.broadcast_to(by_pair[None], (4, 4, 2, 16, HEAD)).reshape(16, 2, 16, HEAD)
+    copies = spread(master_flat.reshape(16 * Z, HEAD))
     far = exchange(copies, far_groups())
     far = jnp.transpose(far, (1, 0, 2, 3))
     copies = jnp.broadcast_to(far[None], (8, 2, 16, 16, HEAD)).reshape(16, 16, 16, HEAD)

time: 56.6 us -> 55.6 us (0.982)
  starting transfers between devices: 6.4 us -> 3.97 us
  blocking collectives: 44.2 us -> 45.6 us
  Pallas kernels: 1.81 us -> 2.67 us
  other arithmetic: 1 us -> 0.16 us
    ppermute x1, starting transfers between devices: 6.4 us -> 3.97 us  [shards(): other = lax.ppermute(own, 'c', [(0, 1), (1, 0)])]
    all_to_all x2, blocking collectives: 44.2 us -> 45.6 us  [exchange(): lax.all_to_all(blocks, AXES, 0, 0, axis_index_groups=groups, tiled=True)]
    pallas_call x0 -> x1, Pallas kernels: none -> 0.87 us  [spread(): pl.pallas_call(spread_kernel, in_specs=[vmem], out_specs=vmem, out_shape=...]
    transpose x1 -> x0, other arithmetic: 0.85 us -> none  [shards(): by_channel = jnp.transpose(rounded, (1, 0, 2))]
where the time goes in v5:
time: 55.6 us; the launch traced here: 55.4 us
  blocking collectives  45.6 us (82%)
  starting transfers between devices  3.97 us (7%)
  Pallas kernels  2.67 us (5%)
  waiting for transfers between devices  2.11 us (4%)
  between operations  0.65 us (1%)
    all_to_all x2, blocking collectives, exchange(): lax.all_to_all(blocks, AXES, 0, 0, axis_index_groups=groups, tiled=True)  45.6 us
    ppermute x1, starting transfers between devices, shards(): other = lax.ppermute(own, 'c', [(0, 1), (1, 0)])  3.97 us
    ppermute x1, waiting for transfers between devices, shards(): other = lax.ppermute(own, 'c', [(0, 1), (1, 0)])  2.11 us
    pallas_call x1, Pallas kernels, finish(): pl.pallas_call(finish_kernel, in_specs=[vmem, vmem, vmem], out_specs=[pl....  1.81 us
  transfers between devices with their start and end apart: 1, of which 1 were waited for; matrix products, arithmetic and copies ran while one was open for 0% of the time, Pallas kernels for 0%

profile of v5, /device:TPU:1, one launch (start us, length us, event | category | flops | bytes accessed | tf_op | source)
XLA Modules:
  0.0 55.4 jit_solution(7426214885536362437)
XLA Ops:
  0.6 0.9 %spread.1 = bf16[16,2,16,128]{3,2,1,0:T(8,128)(2,1)S(1)} custom-call(f32[128,128]{1,0:T(8,128)} %bitcast.11), custom_call_target="tpu_custom_call" | custom-call | tf_op jit(solution)/shard_map/spread/pallas_call | solution.py:102
  1.5 27.7 %all_to_all.10 = bf16[16,2,16,128]{3,2,1,0:T(8,128)(2,1)S(1)} all-to-all(bf16[16,2,16,128]{3,2,1,0:T(8,128)(2,1)S(1)} %spread.1), channel_id=1, replica_groups={{0,2,4,6,32,34,36,38,64,66,68,70,96,98,100,102},{1,3,5,7,33,35,37,39,65..., dimensions={0} | all-to-all | bytes 262144 | tf_op jit(solution)/shard_map/all_to_all | solution.py:40
  29.2 0.2 broadcast_in_dim.4
  29.4 17.9 %all_to_all.11 = bf16[16,16,16,128]{3,2,1,0:T(8,128)(2,1)S(1)} all-to-all(bf16[16,16,16,128]{3,2,1,0:T(8,128)(2,1)S(1)} %bitcast.9), channel_id=1, replica_groups={{0,1,16,17,128,129,144,145,256,257,272,273,384,385,400,401},{2,3,18,19,..., dimensions={0} | all-to-all | bytes 2097152 | tf_op jit(solution)/shard_map/all_to_all | solution.py:40
  47.3 4.0 %collective-permute-start = (bf16[64,4,16,128]{3,2,1,0:T(8,128)(2,1)S(1)}, bf16[64,4,16,128]{3,2,1,0:T(8,128)(2,1)S(1)}, u32[]{:S(2)}, u32[]{:S(2)}) collective-permute-start(bf16[64,4,16,128]{3,2,1,0:T(8,128)(2,1)S(1)} %bitcast.6), channel_id=1, source_target_pairs={{0,8},{8,0},{1,9},{9,1},{2,10},{10,2},{3,11},{11,3},{4,12},{12,4},... | collective-permute-start | bytes 3145736 | tf_op jit(solution)/shard_map/ppermute | solution.py:117
  51.3 0.2 abs_reduce_fusion
  51.4 2.1 %collective-permute-done.other_ref = bf16[64,4,16,128]{3,2,1,0:T(8,128)(2,1)S(1)} collective-permute-done((bf16[64,4,16,128]{3,2,1,0:T(8,128)(2,1)S(1)}, bf16[64,4,16,128]{3,2,1,0:T(8,128)(2,1)S(1)}, u32[]{:S(2)}, u32[]{:S(2)}) %collective-permute-start) | collective-permute-done | bytes 1048608 | tf_op jit(solution)/shard_map/ppermute | solution.py:117
  53.6 1.8 %finish.1 = (bf16[32,2,4,2,16,128]{5,4,3,2,1,0:T(8,128)(2,1)}, f32[1,128]{1,0:T(1,128)}) custom-call(bf16[1,128]{1,0:T(2,128)(2,1)S(1)} %bitcast.8, bf16[64,4,16,128]{3,2,1,0:T(8,128)(2,1)S(1)} %bitcast.7, bf16[64,4,16,128]{3,2,1,0:T(8,128)(2,1)S(1)} %collective-permute-done.other_ref), custom_call_target="tpu_custom_call" | custom-call | tf_op jit(solution)/shard_map/finish/pallas_call | solution.py:72
  (1 shorter events, 0.0 us)
Async XLA Ops:
  47.3 6.2 %collective-permute-start = (bf16[64,4,16,128]{3,2,1,0:T(8,128)(2,1)S(1)}, bf16[64,4,16,128]{3,2,1,0:T(8,128)(2,1)S(1)}, u32[]{:S(2)}, u32[]{:S(2)}) collective-permute-start(bf16[64,4,16,128]{3,2,1,0:T(8,128)(2,1)S(1)} %bitcast.6), channel_id=1, source_target_pairs={{0,8},{8,0},{1,9},{9,1},{2,10},{10,2},{3,11},{11,3},{4,12},{12,4},... | collective-permute-start | bytes 3145736 | tf_op jit(solution)/shard_map/ppermute | solution.py:117
